TPU v7x, 128 devices: a whole 4x4x4 slice. The times are simulated.
128 devices in a mesh: dp: 4 (over z), mp: 32 (over y, x, core).
Axes of the slice: x: 4, y: 4, z: 4, core: 2. Of those that a mesh axis runs over, the one named last changes fastest.
Arguments:
- tokens: bfloat16 [4096, 4096], P('dp', 'mp'), may hold values from -6 to 6
- decay: float32 [4096, 16], P('dp'), may hold values from 0.75 to 1, as said below
- state: float32 [128, 256, 8192], P('dp', None, 'mp'), may hold values from -24 to 24
- w_query: bfloat16 [4096, 4096], P(None, 'mp'), may hold values from -0.09375 to 0.09375
- w_key: bfloat16 [4096, 4096], P(None, 'mp'), may hold values from -0.09375 to 0.09375
- w_value: bfloat16 [4096, 8192], P(None, 'mp'), may hold values from -0.09375 to 0.09375
- w_gate: bfloat16 [4096, 8192], P(None, 'mp'), may hold values from -0.09375 to 0.09375
- w_out: bfloat16 [8192, 4096], P('mp'), may hold values from -0.125 to 0.125
- norm_gain: float32 [8192], P('mp'), may hold values from 0.25 to 1.75
Outputs:
- layer_out: bfloat16 [4096, 4096], P('dp', 'mp')
- new_state: float32 [128, 256, 8192], P('dp', None, 'mp')
Inputs may be any that keep to these rules, and one draw needn't show every extreme that they name: `decay`: each head has its own base rate over all tokens, varied somewhat from token to token.
All inputs are finite; a program needn't handle non-finite values.
Results may differ from a plain program's by a relative error of at most 0.0071.
Values may be sent and summed in bfloat16 or wider, within the bound.
No kernel may reach another device: no remote copies, remote signals or barrier semaphores. Data moves between devices by JAX's collectives and lax.ppermute only.
A program may use at most 128 MiB of HBM per device.

v0:
```python
import jax
import jax.numpy as jnp
from jax import lax
from jax.sharding import PartitionSpec as P

HEAD = 256
VHEAD = 512
NEW = 32
EPS = 0.1


def partner(shard, axis, bit):
    return lax.ppermute(shard, axis, [(i, i ^ 1 << bit) for i in range(lax.axis_size(axis))])


def per_device(tokens, decay, state, w_query, w_key, w_value, w_gate, w_out, norm_gain):
    tok_rows = tokens.shape[0]
    qk_columns = w_query.shape[1]
    v_columns = w_value.shape[1]
    groups = max(1, qk_columns // HEAD)
    qk_width = qk_columns // groups
    v_width = v_columns // groups
    sequences = tok_rows // NEW
    device_index = lax.axis_index("mp")
    first_head = device_index * qk_columns // HEAD
    qk_zeros = jnp.zeros((tok_rows, qk_columns), jnp.float32)
    v_zeros = jnp.zeros((tok_rows, v_columns), jnp.float32)
    carried = (qk_zeros, qk_zeros, v_zeros, v_zeros)
    segment = lax.all_gather(tokens, "mp", axis=1, tiled=True)
    updated = []
    for running, weight in zip(carried, (w_query, w_key, w_value, w_gate)):
        weight_rows = weight
        updated.append(jnp.dot(segment, weight_rows, preferred_element_type=jnp.float32))
    query, key_proj, value_proj, gate_proj = tuple(updated)
    query = (query * HEAD ** (-0.5)).astype(jnp.bfloat16).reshape(tok_rows, groups, qk_width)
    key_proj = key_proj.astype(jnp.bfloat16).reshape(tok_rows, groups, qk_width)
    value_proj = value_proj.astype(jnp.bfloat16)
    bit_number = 0
    other_query, other_key = partner((query, key_proj), "mp", bit_number)
    upper_half = device_index >> bit_number & 1 == 1
    query = jnp.where(
        upper_half,
        jnp.concatenate([other_query, query], 2),
        jnp.concatenate([query, other_query], 2),
    )
    key_proj = jnp.where(
        upper_half,
        jnp.concatenate([other_key, key_proj], 2),
        jnp.concatenate([key_proj, other_key], 2),
    )
    query_block = query.reshape(sequences, NEW, groups, HEAD)
    key_block = key_proj.reshape(sequences, NEW, groups, HEAD)
    value_block = value_proj.reshape(sequences, NEW, groups, v_width)
    decay_rates = lax.dynamic_slice_in_dim(decay, first_head, groups, 1).reshape(
        sequences, NEW, groups
    )
    log_cumul = jnp.cumsum(jnp.log(decay_rates), axis=1)
    old_state = state.reshape(sequences, HEAD, groups, v_width)
    from_state = jnp.einsum("bngk,bkgv->bngv", query_block.astype(jnp.float32), old_state)
    scores = jnp.einsum(
        "bngk,bmgk->bgnm", query_block, key_block, preferred_element_type=jnp.float32
    )
    along = jnp.transpose(log_cumul, (0, 2, 1))
    log_gap = along[:, :, :, None] - along[:, :, None, :]
    causal = jnp.arange(NEW)[:, None] >= jnp.arange(NEW)[None, :]
    factor = jnp.where(causal, jnp.exp(jnp.where(causal, log_gap, 0.0)), 0.0)
    weights = (scores * factor).astype(jnp.bfloat16)
    in_block = jnp.einsum(
        "bgnm,bmgv->bngv", weights, value_block, preferred_element_type=jnp.float32
    )
    retained = jnp.exp(log_cumul)[..., None] * from_state + in_block
    final_log = log_cumul[:, -1, :]
    carry_scale = jnp.exp(final_log[:, None, :] - log_cumul)
    decayed_keys = key_block.astype(jnp.float32) * carry_scale[..., None]
    fresh = jnp.einsum("bngk,bngv->bkgv", decayed_keys, value_block.astype(jnp.float32))
    new_state = jnp.exp(final_log)[:, None, :, None] * old_state + fresh
    new_state = new_state.reshape(sequences, HEAD, v_columns)
    retained = retained.reshape(tok_rows, groups, v_width)
    running = jnp.sum(retained, axis=-1)
    squares = jnp.sum(retained * retained, axis=-1)
    bit_number = 0
    other_sum, other_square = partner((running, squares), "mp", bit_number)
    running = running + other_sum
    squares = squares + other_square
    centre = running / VHEAD
    variance = squares / VHEAD - centre * centre
    deviation = retained - centre[..., None]
    normed = deviation * lax.rsqrt(variance + EPS)[..., None]
    gated_out = (normed.reshape(tok_rows, v_columns) * norm_gain * jax.nn.silu(gate_proj)).astype(
        jnp.bfloat16
    )
    out_cols = lax.all_to_all(w_out, "mp", split_axis=1, concat_axis=0, tiled=True)
    weight_rows = out_cols
    layer_out = jnp.dot(
        lax.all_gather(gated_out, "mp", axis=1, tiled=True),
        weight_rows,
        preferred_element_type=jnp.float32,
    ).astype(jnp.bfloat16)
    return (layer_out, new_state)


def solution(mesh):
    placed = (
        P("dp", "mp"),
        P("dp", None),
        P("dp", None, "mp"),
        P(None, "mp"),
        P(None, "mp"),
        P(None, "mp"),
        P(None, "mp"),
        P("mp", None),
        P("mp"),
    )
    return jax.shard_map(
        per_device,
        mesh=mesh,
        in_specs=placed,
        out_specs=(P("dp", "mp"), P("dp", None, "mp")),
        check_vma=False,
    )
```

profile of v0, /device:TPU:1, one launch (start us, length us, event | category | flops | bytes accessed | tf_op | source)
XLA Modules:
  0.0 216.4 jit_solution(17912909884485674575)
XLA Ops:
  7.2 0.0 copy-start
  7.2 0.0 all-gather.3.cloned.1.call-start
  7.2 0.7 all-gather.3.cloned.1.call-update
  7.9 0.0 all-gather.5.cloned.1.call-start
  8.0 0.8 log_reduce_fusion
  8.8 0.1 log.15
  8.8 0.5 copy.22
  9.4 2.0 fusion.26
  11.4 0.4 copy.23
  11.7 0.1 slice_reduce_fusion
  11.9 0.1 subtract_exponential_fusion
  11.9 60.5 %all-gather.3.cloned.1.call-done = bf16[1024,4096]{1,0:T(8,128)(2,1)} async-done(((bf16[1024,128]{1,0:T(8,128)(2,1)}), bf16[1024,4096]{1,0:T(8,128)(2,1)}) %all-gather.3.cloned.1.call-update) | async-done | bytes 8388624 | tf_op jit(solution)/shard_map/all_gather | solution.py:29
  72.5 6.1 %fusion.4 = bf16[1024,128]{1,0:T(8,128)(2,1)S(1)} fusion(bf16[1024,4096]{1,0:T(8,128)(2,1)} %all-gather.3.cloned.1.call-done, bf16[4096,128]{1,0:T(8,128)(2,1)} %param.12), kind=kOutput, calls=%fused_computation.11 | convolution fusion | flops 1074003968 | bytes 9699328 | tf_op jit(solution)/shard_map/dot_general | solution.py:33
  78.5 0.3 collective-permute-start
  78.9 0.0 copy-done.10
  78.9 0.0 copy-done.11
  78.9 2.3 %convolution_convert_fusion.2 = bf16[1024,128]{1,0:T(8,128)(2,1)S(1)} fusion(bf16[1024,4096]{1,0:T(8,128)(2,1)S(1)} %copy-done.10, bf16[4096,128]{1,0:T(8,128)(2,1)S(1)} %copy-done.11), kind=kOutput, calls=%fused_computation.12 | convolution fusion | flops 1073872896 | bytes 9699328 | tf_op jit(solution)/shard_map/dot_general | solution.py:33
  81.2 0.0 copy-start.6
  81.2 0.3 collective-permute-start.1
  81.6 0.0 copy-done
  81.6 2.3 %convolution_convert_fusion = bf16[1024,256]{1,0:T(8,128)(2,1)S(1)} fusion(bf16[1024,4096]{1,0:T(8,128)(2,1)S(1)} %copy-done.10, bf16[4096,256]{1,0:T(8,128)(2,1)S(1)} %copy-done), kind=kOutput, calls=%fused_computation.6 | convolution fusion | flops 2147745792 | bytes 11010048 | tf_op jit(solution)/shard_map/dot_general | solution.py:33
  83.9 0.0 collective-permute-done
  83.9 0.0 copy-start.5
  83.9 0.0 collective-permute-done.1
  84.0 0.0 copy-start.8
  84.0 0.8 copy-done.8
  84.7 1.5 convolution_bitcast_fusion
  86.3 4.5 %fusion.9 = (f32[32,32]{1,0:T(8,128)S(1)}, f32[32,32]{1,0:T(8,128)S(1)}, f32[32,1,256,32]{2,3,0,1:T(8,128)S(1)}) fusion(f32[32,1,256,32]{2,3,0,1:T(8,128)S(1)} %convolution_bitcast_fusion, f32[32,256,256]{2,1,0:T(8,128)} %param.11, bf16[32,32,128]{2,1,0:T(8,128)(2,1)S(1)} %bitcast.72, bf16[32,32,128]{2,1,0:T(8,128)(2,1)} %bitcast.74, pred[]{:T(512)S(6)} %eq.3, ...), kind=kOutput, calls=%fused_computation.20 | convolution fusion | flops 137885696 | bytes 11022337 | tf_op jit(solution)/shard_map/bngk,bkgv->bngv/dot_general | solution.py:59
  90.8 0.1 reduce_sum.25
  90.9 0.1 reduce_sum.23
  91.0 0.3 collective-permute-start.2
  91.3 0.2 collective-permute-start.3
  91.5 0.7 collective-permute-done.2
  92.2 0.3 collective-permute-done.3
  92.5 0.0 copy-start.2
  92.5 7.4 %fusion.8 = bf16[1024,256]{1,0:T(8,128)(2,1)} fusion(f32[32,1,256,32]{2,3,0,1:T(8,128)S(1)} %get-tuple-element.14, f32[256]{0:T(256)S(1)} %copy-done.12, f32[1024]{0:T(1024)S(1)} %bitcast.81, f32[1024]{0:T(1024)S(1)} %bitcast.82, bf16[1024,4096]{1,0:T(8,128)(2,1)} %all-gather.3.cloned.1.call-done, bf16[4096,256]{1,0:T(8,128)(2,1)} %param.15), kind=kOutput, calls=%fused_computation.17 | convolution fusion | flops 2149842944 | bytes 12067840 | tf_op jit(solution)/shard_map/dot_general | solution.py:33
  99.9 0.0 all-gather.5.cloned.1.call-update
  99.9 2.5 %copy.24 = bf16[256,4096]{0,1:T(8,128)(2,1)} copy(bf16[256,4096]{1,0:T(8,128)(2,1)S(1)} %copy-done.2) | data formatting | bytes 4194304 | tf_op args[7]
  102.4 5.6 %all-to-all-start = ((bf16[256,32,128]{0,2,1:T(8,128)(2,1)}), bf16[256,32,128]{0,2,1:T(8,128)(2,1)S(1)}, u32[]{:S(2)}, u32[]{:S(2)}) async-start(bf16[256,32,128]{0,2,1:T(8,128)(2,1)} %bitcast.66), calls=%async_computation | async-start | bytes 4194304 | tf_op jit(solution)/shard_map/all_to_all | solution.py:92
  108.0 0.0 copy-start.9
  108.0 9.2 %copy.26 = f32[32,256,256]{1,2,0:T(8,128)} copy(f32[32,256,256]{2,1,0:T(8,128)} %param.11) | data formatting | bytes 16777216 | tf_op args[2]
  117.2 27.7 %all-to-all-done = bf16[256,32,128]{0,2,1:T(8,128)(2,1)S(1)} async-done(((bf16[256,32,128]{0,2,1:T(8,128)(2,1)}), bf16[256,32,128]{0,2,1:T(8,128)(2,1)S(1)}, u32[]{:S(2)}, u32[]{:S(2)}) %all-to-all-start) | async-done | bytes 2097184 | tf_op jit(solution)/shard_map/all_to_all | solution.py:92
  144.9 2.9 %copy.25 = bf16[32,256,128]{2,1,0:T(8,128)(2,1)} copy(bf16[32,256,128]{1,2,0:T(8,128)(2,1)S(1)} %bitcast.65) | data formatting | bytes 4194304 | tf_op jit(solution)/shard_map/all_to_all | solution.py:92
  147.8 0.0 copy-done.7
  147.8 8.5 %fusion = f32[32,256,256]{1,2,0:T(8,128)} fusion(f32[32,256,256]{1,2,0:T(8,128)} %copy.26, f32[32]{0:T(128)S(1)} %exp.38, bf16[32,32,256]{2,1,0:T(8,128)(2,1)S(1)} %bitcast.69, f32[32,32]{1,0:T(8,128)S(1)} %get-tuple-element.12, bf16[32,32,128]{2,1,0:T(8,128)(2,1)S(1)} %bitcast.77, bf16[32,32,128]{2,1,0:T(8,128)(2,1)S(1)} %bitcast.79, pred[]{:T(512)S(6)} %eq.3), kind=kOutput, calls=%fused_computation.1 | convolution fusion | flops 141295616 | bytes 17830016 | tf_op jit(solution)/shard_map/bngk,bngv->bkgv/dot_general | solution.py:75
  156.3 9.0 %copy.27 = f32[32,256,256]{2,1,0:T(8,128)} copy(f32[32,256,256]{1,2,0:T(8,128)} %fusion) | data formatting | bytes 16777216
  165.3 32.6 %all-gather.5.cloned.1.call-done = bf16[1024,8192]{1,0:T(8,128)(2,1)} async-done(((bf16[1024,256]{1,0:T(8,128)(2,1)}), bf16[1024,8192]{1,0:T(8,128)(2,1)}) %all-gather.5.cloned.1.call-update) | async-done | bytes 16777232 | tf_op jit(solution)/shard_map/all_gather | solution.py:95
  197.9 11.7 %convolution_convert_fusion.1 = bf16[1024,128]{1,0:T(8,128)(2,1)} fusion(bf16[1024,8192]{1,0:T(8,128)(2,1)} %all-gather.5.cloned.1.call-done, bf16[8192,128]{1,0:T(8,128)(2,1)} %bitcast.67), kind=kOutput, calls=%fused_computation.9 | convolution fusion | flops 2147614720 | bytes 19136512 | tf_op jit(solution)/shard_map/dot_general | solution.py:94
  (18 shorter events, 0.1 us)
Async XLA Ops:
  7.2 74.4 %copy-start = (bf16[4096,256]{1,0:T(8,128)(2,1)S(1)}, bf16[4096,256]{1,0:T(8,128)(2,1)}, u32[]{:S(2)}) copy-start(bf16[4096,256]{1,0:T(8,128)(2,1)} %param.14) | copy-start | bytes 6291460
  7.2 65.3 %all-gather.3.cloned.1.call-start = ((), (), s32[]{:S(2)}) async-start(), calls=%async_computation.1 | async-start | bytes 8650752 | tf_op jit(solution)/shard_map/all_gather | solution.py:29
  7.9 190.0 %all-gather.5.cloned.1.call-start = ((), (), s32[]{:S(2)}) async-start(), calls=%async_computation.2 | async-start | bytes 17301504 | tf_op jit(solution)/shard_map/all_gather | solution.py:95
  72.5 6.4 %copy-start.10 = (bf16[1024,4096]{1,0:T(8,128)(2,1)S(1)}, bf16[1024,4096]{1,0:T(8,128)(2,1)}, u32[]{:S(2)}) copy-start(bf16[1024,4096]{1,0:T(8,128)(2,1)} %all-gather.3.cloned.1.call-done) | copy-start | bytes 25165828
  72.5 6.4 %copy-start.11 = (bf16[4096,128]{1,0:T(8,128)(2,1)S(1)}, bf16[4096,128]{1,0:T(8,128)(2,1)}, u32[]{:S(2)}) copy-start(bf16[4096,128]{1,0:T(8,128)(2,1)} %param.13) | copy-start | bytes 3145732
  78.5 5.4 %collective-permute-start = (bf16[1024,1,128]{2,0,1:T(8,128)(2,1)S(1)}, bf16[1024,1,128]{2,0,1:T(8,128)(2,1)S(1)}, u32[]{:S(2)}, u32[]{:S(2)}) collective-permute-start(bf16[1024,1,128]{2,0,1:T(8,128)(2,1)S(1)} %bitcast.70), channel_id=1, source_target_pairs={{0,1},{1,0},{2,3},{3,2},{4,5},{5,4},{6,7},{7,6},{8,9},{9,8},{10,11... | collective-permute-start | bytes 786440 | tf_op jit(solution)/shard_map/ppermute | solution.py:13
  81.2 5.0 %copy-start.6 = (bf16[1024,128]{1,0:T(8,128)(2,1)}, bf16[1024,128]{1,0:T(8,128)(2,1)S(1)}, u32[]{:S(2)}) copy-start(bf16[1024,128]{1,0:T(8,128)(2,1)S(1)} %convolution_convert_fusion.2) | copy-start | bytes 786436
  81.2 2.7 %collective-permute-start.1 = (bf16[1024,1,128]{2,0,1:T(8,128)(2,1)S(1)}, bf16[1024,1,128]{2,0,1:T(8,128)(2,1)S(1)}, u32[]{:S(2)}, u32[]{:S(2)}) collective-permute-start(bf16[1024,1,128]{2,0,1:T(8,128)(2,1)S(1)} %bitcast.75), channel_id=1, source_target_pairs={{0,1},{1,0},{2,3},{3,2},{4,5},{5,4},{6,7},{7,6},{8,9},{9,8},{10,11... | collective-permute-start | bytes 786440 | tf_op jit(solution)/shard_map/ppermute | solution.py:13
  83.9 2.4 %copy-start.3 = (bf16[1024,256]{1,0:T(8,128)(2,1)}, bf16[1024,256]{1,0:T(8,128)(2,1)S(1)}, u32[]{:S(2)}) copy-start(bf16[1024,256]{1,0:T(8,128)(2,1)S(1)} %convolution_convert_fusion) | copy-start | bytes 1572868
  83.9 2.4 %copy-start.5 = (bf16[1024,1,128]{2,0,1:T(8,128)(2,1)}, bf16[1024,1,128]{2,0,1:T(8,128)(2,1)S(1)}, u32[]{:S(2)}) copy-start(bf16[1024,1,128]{2,0,1:T(8,128)(2,1)S(1)} %collective-permute-done) | copy-start | bytes 786436
  84.0 0.8 copy-start.8
  84.7 7.8 %copy-start.12 = (f32[256]{0:T(256)S(1)}, f32[256]{0:T(256)}, u32[]{:S(2)}) copy-start(f32[256]{0:T(256)} %param.17) | copy-start | bytes 3076
  91.0 1.2 collective-permute-start.2
  91.3 1.2 collective-permute-start.3
  92.5 7.4 %copy-start.2 = (bf16[256,4096]{1,0:T(8,128)(2,1)S(1)}, bf16[256,4096]{1,0:T(8,128)(2,1)}, u32[]{:S(2)}) copy-start(bf16[256,4096]{1,0:T(8,128)(2,1)} %param.16) | copy-start | bytes 6291460
  102.4 42.5 %all-to-all-start = ((bf16[256,32,128]{0,2,1:T(8,128)(2,1)}), bf16[256,32,128]{0,2,1:T(8,128)(2,1)S(1)}, u32[]{:S(2)}, u32[]{:S(2)}) async-start(bf16[256,32,128]{0,2,1:T(8,128)(2,1)} %bitcast.66), calls=%async_computation | async-start | bytes 4194304 | tf_op jit(solution)/shard_map/all_to_all | solution.py:92
  108.0 39.8 %copy-start.4 = (bf16[1024,256]{1,0:T(8,128)(2,1)S(1)}, bf16[1024,256]{1,0:T(8,128)(2,1)}, u32[]{:S(2)}) copy-start(bf16[1024,256]{1,0:T(8,128)(2,1)} %copy-done.3) | copy-start | bytes 1572868
  108.0 39.8 %copy-start.7 = (bf16[1024,128]{1,0:T(8,128)(2,1)S(1)}, bf16[1024,128]{1,0:T(8,128)(2,1)}, u32[]{:S(2)}) copy-start(bf16[1024,128]{1,0:T(8,128)(2,1)} %copy-done.6) | copy-start | bytes 786436
  108.0 39.8 %copy-start.9 = (bf16[1024,1,128]{2,0,1:T(8,128)(2,1)S(1)}, bf16[1024,1,128]{2,0,1:T(8,128)(2,1)}, u32[]{:S(2)}) copy-start(bf16[1024,1,128]{2,0,1:T(8,128)(2,1)} %copy-done.8) | copy-start | bytes 786436
  197.9 11.7 %copy-start.1 = (bf16[4096,256]{1,0:T(8,128)(2,1)S(1)}, bf16[4096,256]{1,0:T(8,128)(2,1)}, u32[]{:S(2)}) copy-start(bf16[4096,256]{1,0:T(8,128)(2,1)} %param.14) | copy-start | bytes 6291460
Sparse Core Ops, SparseCore 0:
  10.2 62.2 all-gather.2
  100.0 97.8 all-gather.4
where the time goes:
time: 217 us; the launch traced here: 216 us
  waiting for transfers between devices  122 us (56%)
  matrix products  44.4 us (20%)
  local copies, waits for them, and re-layouts  26.4 us (12%)
  between operations  14.3 us (7%)
  starting transfers between devices  6.87 us (3%)
    all_gather x1, waiting for transfers between devices, per_device(): segment = lax.all_gather(tokens, 'mp', axis=1, tiled=True)  60.5 us
    all_gather x1, waiting for transfers between devices, per_device(): lax.all_gather(gated_out, 'mp', axis=1, tiled=True)  32.6 us
    all_to_all x1, waiting for transfers between devices, per_device(): lax.all_to_all(w_out, 'mp', split_axis=1, concat_axis=0, tiled=True)  27.7 us
    unnamed x29, local copies, waits for them, and re-layouts  21.5 us
    dot_general x4, matrix products, per_device(): jnp.dot(segment, weight_rows, preferred_element_type=jnp.float32)  18.1 us
    dot_general x1, matrix products, per_device(): jnp.dot(lax.all_gather(gated_out, 'mp', axis=1, tiled=True), weight_rows,...  11.7 us
    dot_general x1, matrix products, per_device(): jnp.einsum('bngk,bngv->bkgv', decayed_keys, value_block.astype(jnp.float32))  8.48 us
    all_to_all x1, starting transfers between devices, per_device(): lax.all_to_all(w_out, 'mp', split_axis=1, concat_axis=0, tiled=True)  5.6 us
  transfers between devices with their start and end apart: 7, of which 5 were waited for; matrix products, arithmetic and copies ran while one was open for 19% of the time, Pallas kernels for 0%

commit v1 on v0

--- a/solution.py
+++ b/solution.py
@@ -7,6 +7,14 @@
 VHEAD = 512
 NEW = 32
 EPS = 0.1
+
+
+def gather_by_exchange(array, axis, dim):
+    devices = lax.axis_size(axis)
+    repeats = [devices if d == dim else 1 for d in range(array.ndim)]
+    return lax.all_to_all(
+        jnp.tile(array, repeats), axis, split_axis=dim, concat_axis=dim, tiled=True
+    )
 
 
 def partner(shard, axis, bit):
@@ -92,9 +100,7 @@
     out_cols = lax.all_to_all(w_out, "mp", split_axis=1, concat_axis=0, tiled=True)
     weight_rows = out_cols
     layer_out = jnp.dot(
-        lax.all_gather(gated_out, "mp", axis=1, tiled=True),
-        weight_rows,
-        preferred_element_type=jnp.float32,
+        gather_by_exchange(gated_out, "mp", 1), weight_rows, preferred_element_type=jnp.float32
     ).astype(jnp.bfloat16)
     return (layer_out, new_state)
 

time: 217 us -> 360 us (1.66)
  the two profiles are of different devices: /device:TPU:1 before, /device:TPU:0 now
where the time goes in v1:
time: 360 us; the launch traced here: 359 us
  waiting for transfers between devices  250 us (69%)
  matrix products  42.6 us (12%)
  local copies, waits for them, and re-layouts  34.9 us (10%)
  starting transfers between devices  14.7 us (4%)
  between operations  14.2 us (4%)
    all_to_all x1, waiting for transfers between devices, gather_by_exchange(): lax.all_to_all(jnp.tile(array, repeats), axis, split_axis=dim, concat_axi...  187 us
    all_gather x1, waiting for transfers between devices, per_device(): segment = lax.all_gather(tokens, 'mp', axis=1, tiled=True)  61.6 us
    unnamed x17, local copies, waits for them, and re-layouts  22.9 us
    dot_general x4, matrix products, per_device(): jnp.dot(segment, weight_rows, preferred_element_type=jnp.float32)  17.2 us
    dot_general x1, matrix products, per_device(): jnp.dot(gather_by_exchange(gated_out, 'mp', 1), weight_rows, preferred_el...  11.6 us
    dot_general x1, matrix products, per_device(): jnp.einsum('bngk,bngv->bkgv', decayed_keys, value_block.astype(jnp.float32))  7.98 us
    all_to_all x1, starting transfers between devices, per_device(): lax.all_to_all(w_out, 'mp', split_axis=1, concat_axis=0, tiled=True)  7.56 us
  transfers between devices with their start and end apart: 7, of which 4 were waited for; matrix products, arithmetic and copies ran while one was open for 17% of the time, Pallas kernels for 0%

profile of v1, /device:TPU:0, one launch (start us, length us, event | category | flops | bytes accessed | tf_op | source)
XLA Modules:
  0.0 358.9 jit_solution(8647165997242104566)
XLA Ops:
  7.2 0.0 copy-start
  7.2 0.0 all-gather.2.cloned.1.call-start
  7.2 0.7 all-gather.2.cloned.1.call-update
  7.9 4.1 %copy.20 = bf16[256,4096]{0,1:T(8,128)(2,1)} copy(bf16[256,4096]{1,0:T(8,128)(2,1)} %param.16) | data formatting | bytes 4194304 | tf_op args[7]
  12.0 4.1 %copy.21 = bf16[256,32,128]{2,0,1:T(8,128)(2,1)} copy(bf16[256,32,128]{0,2,1:T(8,128)(2,1)} %bitcast.73) | data formatting | bytes 4194304 | tf_op jit(solution)/shard_map/all_to_all | solution.py:100
  16.0 7.6 %all-to-all-start.1 = ((bf16[256,32,128]{2,0,1:T(8,128)(2,1)}), bf16[256,32,128]{2,0,1:T(8,128)(2,1)}, u32[]{:S(2)}, u32[]{:S(2)}) async-start(bf16[256,32,128]{2,0,1:T(8,128)(2,1)} %copy.21), calls=%async_computation.1 | async-start | bytes 4194304 | tf_op jit(solution)/shard_map/all_to_all | solution.py:100
  23.6 0.8 log_reduce_fusion
  24.4 0.1 log.15
  24.5 0.5 copy.18
  25.0 2.0 fusion.34
  27.0 0.4 copy.19
  27.4 0.1 slice_reduce_fusion
  27.5 0.1 subtract_exponential_fusion
  27.6 61.6 %all-gather.2.cloned.1.call-done = bf16[1024,4096]{1,0:T(8,128)(2,1)} async-done(((bf16[1024,128]{1,0:T(8,128)(2,1)}), bf16[1024,4096]{1,0:T(8,128)(2,1)}) %all-gather.2.cloned.1.call-update) | async-done | bytes 8388624 | tf_op jit(solution)/shard_map/all_gather | solution.py:37
  89.2 0.0 copy-start.4
  89.2 6.1 %convolution_convert_fusion.1 = bf16[1024,128]{1,0:T(8,128)(2,1)S(1)} fusion(bf16[1024,4096]{1,0:T(8,128)(2,1)} %all-gather.2.cloned.1.call-done, bf16[4096,128]{1,0:T(8,128)(2,1)} %param.13), kind=kOutput, calls=%fused_computation.14 | convolution fusion | flops 1073872896 | bytes 9699328 | tf_op jit(solution)/shard_map/dot_general | solution.py:41
  95.3 0.3 collective-permute-start.1
  95.6 0.0 copy-done.4
  95.6 0.0 copy-done.5
  95.6 2.3 fusion.9
  97.9 0.3 collective-permute-start
  98.3 0.0 copy-done
  98.3 2.3 convolution_convert_fusion
  100.6 0.0 collective-permute-done.1
  100.6 0.0 copy-start.2
  100.6 0.0 collective-permute-done
  100.6 0.7 copy-done.2
  101.3 1.6 convolution_bitcast_fusion
  102.9 4.4 %fusion.17 = (f32[32,32]{1,0:T(8,128)S(1)}, f32[32,32]{1,0:T(8,128)S(1)}, f32[32,1,256,32]{2,3,0,1:T(8,128)S(1)}) fusion(f32[32,1,256,32]{2,3,0,1:T(8,128)S(1)} %convolution_bitcast_fusion, f32[32,256,256]{2,1,0:T(8,128)} %param.11, bf16[32,32,128]{2,1,0:T(8,128)(2,1)S(1)} %bitcast.78, bf16[32,32,128]{2,1,0:T(8,128)(2,1)S(1)} %bitcast.80, pred[]{:T(512)S(6)} %eq.3, ...), kind=kOutput, calls=%fused_computation.23 | convolution fusion | flops 137885696 | bytes 11022337 | tf_op jit(solution)/shard_map/bngk,bkgv->bngv/dot_general | solution.py:67
  107.3 0.1 reduce_sum.25
  107.3 0.3 collective-permute-start.3
  107.6 0.1 reduce_sum.23
  107.7 0.5 collective-permute-start.2
  108.1 0.4 collective-permute-done.3
  108.5 0.5 collective-permute-done.2
  109.1 0.0 copy-done.6
  109.1 6.4 %fusion.16 = bf16[1024,256]{1,0:T(8,128)(2,1)S(1)} fusion(f32[32,1,256,32]{2,3,0,1:T(8,128)S(1)} %get-tuple-element.12, f32[256]{0:T(256)S(1)} %copy-done.6, f32[1024]{0:T(1024)S(1)} %bitcast.87, f32[1024]{0:T(1024)S(1)} %bitcast.88, bf16[1024,4096]{1,0:T(8,128)(2,1)} %all-gather.2.cloned.1.call-done, bf16[4096,256]{1,0:T(8,128)(2,1)} %param.15), kind=kOutput, calls=%fused_computation.20 | convolution fusion | flops 2149842944 | bytes 12067840 | tf_op jit(solution)/shard_map/dot_general | solution.py:41
  115.5 0.0 all-to-all-done.1
  115.5 6.0 %tile.2 = bf16[1024,32,256]{2,0,1:T(8,128)(2,1)} broadcast(bf16[1024,256]{1,0:T(8,128)(2,1)S(1)} %fusion.16), dimensions={0,2} | broadcast | bytes 17301504 | tf_op jit(solution)/shard_map/tile | solution.py:16
  121.5 5.7 %all-to-all-start = ((bf16[1024,32,256]{2,0,1:T(8,128)(2,1)}), bf16[1024,32,256]{2,0,1:T(8,128)(2,1)}, u32[]{:S(2)}, u32[]{:S(2)}) async-start(bf16[1024,32,256]{2,0,1:T(8,128)(2,1)} %tile.2), calls=%async_computation | async-start | bytes 33554432 | tf_op jit(solution)/shard_map/all_to_all | solution.py:15
  127.2 0.0 copy-start.3
  127.2 9.0 %copy.22 = f32[32,256,256]{1,2,0:T(8,128)} copy(f32[32,256,256]{2,1,0:T(8,128)} %param.11) | data formatting | bytes 16777216 | tf_op args[2]
  136.2 0.0 copy-done.3
  136.2 8.0 %fusion = f32[32,256,256]{1,2,0:T(8,128)} fusion(f32[32,256,256]{1,2,0:T(8,128)} %copy.22, f32[32]{0:T(128)S(1)} %exp.38, bf16[32,32,256]{2,1,0:T(8,128)(2,1)S(1)} %bitcast.75, f32[32,32]{1,0:T(8,128)S(1)} %get-tuple-element.10, bf16[32,32,128]{2,1,0:T(8,128)(2,1)S(1)} %bitcast.83, bf16[32,32,128]{2,1,0:T(8,128)(2,1)S(1)} %bitcast.85, pred[]{:T(512)S(6)} %eq.3), kind=kOutput, calls=%fused_computation.1 | convolution fusion | flops 141295616 | bytes 17830016 | tf_op jit(solution)/shard_map/bngk,bngv->bkgv/dot_general | solution.py:83
  144.2 9.1 %copy.23 = f32[32,256,256]{2,1,0:T(8,128)} copy(f32[32,256,256]{1,2,0:T(8,128)} %fusion) | data formatting | bytes 16777216
  153.3 187.2 %all-to-all-done = bf16[1024,32,256]{2,0,1:T(8,128)(2,1)} async-done(((bf16[1024,32,256]{2,0,1:T(8,128)(2,1)}), bf16[1024,32,256]{2,0,1:T(8,128)(2,1)}, u32[]{:S(2)}, u32[]{:S(2)}) %all-to-all-start) | async-done | bytes 16777248 | tf_op jit(solution)/shard_map/all_to_all | solution.py:15
  340.5 11.6 %fusion.10 = bf16[1024,128]{1,0:T(8,128)(2,1)} fusion(bf16[1024,32,256]{2,0,1:T(8,128)(2,1)} %all-to-all-done, bf16[256,32,128]{2,0,1:T(8,128)(2,1)} %all-to-all-done.1), kind=kOutput, calls=%fused_computation.15 | convolution fusion | flops 2147614720 | bytes 19136512 | tf_op jit(solution)/shard_map/dot_general | solution.py:102
  352.0 0.0 copy-done.1
  (6 shorter events, 0.0 us)
Async XLA Ops:
  7.2 91.1 %copy-start = (bf16[4096,256]{1,0:T(8,128)(2,1)S(1)}, bf16[4096,256]{1,0:T(8,128)(2,1)}, u32[]{:S(2)}) copy-start(bf16[4096,256]{1,0:T(8,128)(2,1)} %param.14) | copy-start | bytes 6291460
  7.2 82.0 %all-gather.2.cloned.1.call-start = ((), (), s32[]{:S(2)}) async-start(), calls=%async_computation.2 | async-start | bytes 8650752 | tf_op jit(solution)/shard_map/all_gather | solution.py:37
  16.0 99.5 %all-to-all-start.1 = ((bf16[256,32,128]{2,0,1:T(8,128)(2,1)}), bf16[256,32,128]{2,0,1:T(8,128)(2,1)}, u32[]{:S(2)}, u32[]{:S(2)}) async-start(bf16[256,32,128]{2,0,1:T(8,128)(2,1)} %copy.21), calls=%async_computation.1 | async-start | bytes 4194304 | tf_op jit(solution)/shard_map/all_to_all | solution.py:100
  89.2 6.4 %copy-start.4 = (bf16[1024,4096]{1,0:T(8,128)(2,1)S(1)}, bf16[1024,4096]{1,0:T(8,128)(2,1)}, u32[]{:S(2)}) copy-start(bf16[1024,4096]{1,0:T(8,128)(2,1)} %all-gather.2.cloned.1.call-done) | copy-start | bytes 25165828
  89.2 6.4 %copy-start.5 = (bf16[4096,128]{1,0:T(8,128)(2,1)S(1)}, bf16[4096,128]{1,0:T(8,128)(2,1)}, u32[]{:S(2)}) copy-start(bf16[4096,128]{1,0:T(8,128)(2,1)} %param.12) | copy-start | bytes 3145732
  95.3 5.4 %collective-permute-start.1 = (bf16[1024,1,128]{2,0,1:T(8,128)(2,1)S(1)}, bf16[1024,1,128]{2,0,1:T(8,128)(2,1)S(1)}, u32[]{:S(2)}, u32[]{:S(2)}) collective-permute-start(bf16[1024,1,128]{2,0,1:T(8,128)(2,1)S(1)} %bitcast.81), channel_id=1, source_target_pairs={{0,1},{1,0},{2,3},{3,2},{4,5},{5,4},{6,7},{7,6},{8,9},{9,8},{10,11... | collective-permute-start | bytes 786440 | tf_op jit(solution)/shard_map/ppermute | solution.py:21
  97.9 2.7 collective-permute-start
  100.6 0.7 copy-start.2
  101.3 7.7 %copy-start.6 = (f32[256]{0:T(256)S(1)}, f32[256]{0:T(256)}, u32[]{:S(2)}) copy-start(f32[256]{0:T(256)} %param.17) | copy-start | bytes 3076
  107.3 1.2 collective-permute-start.3
  107.7 1.4 collective-permute-start.2
  121.5 219.0 %all-to-all-start = ((bf16[1024,32,256]{2,0,1:T(8,128)(2,1)}), bf16[1024,32,256]{2,0,1:T(8,128)(2,1)}, u32[]{:S(2)}, u32[]{:S(2)}) async-start(bf16[1024,32,256]{2,0,1:T(8,128)(2,1)} %tile.2), calls=%async_computation | async-start | bytes 33554432 | tf_op jit(solution)/shard_map/all_to_all | solution.py:15
  127.2 9.0 %copy-start.3 = (bf16[1024,1,128]{2,0,1:T(8,128)(2,1)S(1)}, bf16[1024,1,128]{2,0,1:T(8,128)(2,1)}, u32[]{:S(2)}) copy-start(bf16[1024,1,128]{2,0,1:T(8,128)(2,1)} %copy-done.2) | copy-start | bytes 786436
  144.2 207.8 %copy-start.1 = (bf16[4096,256]{1,0:T(8,128)(2,1)S(1)}, bf16[4096,256]{1,0:T(8,128)(2,1)}, u32[]{:S(2)}) copy-start(bf16[4096,256]{1,0:T(8,128)(2,1)} %param.14) | copy-start | bytes 6291460
Sparse Core Ops, SparseCore 0:
  10.2 78.9 all-gather.1
